TPU v7x, 8 devices: a whole 2x2x1 slice. The times are simulated.
8 devices in a mesh: sp: 8 (over z, y, x, core).
Axes of the slice: x: 2, y: 2, z: 1, core: 2. Of those that a mesh axis runs over, the one named last changes fastest.
Arguments:
- x: bfloat16 [8, 2048, 1536], P(None, 'sp')
- ln1_w: bfloat16 [1536], replicated
- w_qkv: bfloat16 [1536, 4608], replicated
- q_ln_w: bfloat16 [16, 96], replicated
- k_ln_w: bfloat16 [16, 96], replicated
- w_out: bfloat16 [1536, 1536], replicated
- grad_y: bfloat16 [8, 2048, 1536], P(None, 'sp')
Outputs:
- output 1: bfloat16 [8, 2048, 1536], P(None, 'sp')
- output 2: bfloat16 [8, 2048, 1536], P(None, 'sp')
- output 3: float32 [1536], replicated
- output 4: float32 [1536, 4608], replicated
- output 5: float32 [16, 96], replicated
- output 6: float32 [16, 96], replicated
- output 7: float32 [1536, 1536], replicated
All inputs are finite; a program needn't handle non-finite values.
Results may differ from a plain program's by a relative error of at most 0.0118169.
Values are sent between devices in bfloat16 or wider.
A program may use at most 1 GiB of HBM per device.

v0:
```python
import math
import jax
import jax.numpy as jnp
from jax import lax
from jax.sharding import PartitionSpec as P


def alibi_slopes(n_heads):
    pow_two = 2 ** math.ceil(math.log2(n_heads))
    exponents = jnp.arange(1, pow_two + 1, dtype=jnp.float32) * (8.0 / pow_two)
    slopes = jnp.exp2(-exponents)
    if pow_two != n_heads:
        slopes = jnp.concatenate([slopes[1::2], slopes[0::2]])[:n_heads]
    return slopes


def layer_norm(values, weight):
    centered = values - jnp.mean(values, axis=-1, keepdims=True)
    var_val = jnp.mean(centered * centered, axis=-1, keepdims=True)
    return centered * lax.rsqrt(var_val + 1e-5) * weight


def block_scores(q_cur, k_all, slopes, q_start, score_scale):
    q_count = q_cur.shape[1]
    k_count = k_all.shape[1]
    scores = jnp.einsum('bqhd,bkhd->bhqk', q_cur, k_all, preferred_element_type=jnp.float32) * score_scale
    pos_gap = (q_start + jnp.arange(q_count))[:, None] - jnp.arange(k_count)[None, :]
    biased = scores - slopes[:, None, None] * pos_gap.astype(jnp.float32)
    return jnp.where(pos_gap >= 0, biased, -1e30)


def attn_forward(q_loc, k_all, v_all, slopes, q_offset, q_blk):
    n_batch, q_len, n_heads, head_dim = q_loc.shape
    n_blk = q_len // q_blk
    score_scale = head_dim ** -0.5
    q_blocks = q_loc.reshape(n_batch, n_blk, q_blk, n_heads, head_dim)

    def one_block(blk_idx):
        q_cur = lax.dynamic_index_in_dim(q_blocks, blk_idx, axis=1, keepdims=False)
        scores = block_scores(q_cur, k_all, slopes, q_offset + blk_idx * q_blk, score_scale)
        row_max = jnp.max(scores, axis=-1)
        weights = jnp.exp(scores - row_max[..., None])
        row_sum = jnp.sum(weights, axis=-1)
        weighted = jnp.einsum('bhqk,bkhd->bqhd', weights.astype(jnp.bfloat16), v_all, preferred_element_type=jnp.float32)
        out_blk = weighted / jnp.swapaxes(row_sum, 1, 2)[..., None]
        return out_blk.astype(jnp.bfloat16), row_max + jnp.log(row_sum)

    out_blocks, lse_blocks = lax.map(one_block, jnp.arange(n_blk))
    out_all = jnp.moveaxis(out_blocks, 0, 1).reshape(n_batch, q_len, n_heads, head_dim)
    return out_all, lse_blocks


def attn_backward(q_loc, k_all, v_all, out_all, d_out, lse_blocks, slopes, q_offset, q_blk):
    n_batch, q_len, n_heads, head_dim = q_loc.shape
    n_blk = q_len // q_blk
    score_scale = head_dim ** -0.5
    q_blocks = q_loc.reshape(n_batch, n_blk, q_blk, n_heads, head_dim)
    do_blocks = d_out.reshape(n_batch, n_blk, q_blk, n_heads, head_dim)
    row_dot = jnp.einsum('bqhd,bqhd->bhq', d_out, out_all, preferred_element_type=jnp.float32).reshape(n_batch, n_heads, n_blk, q_blk)

    def one_block(acc_pair, blk_idx):
        dk_acc, dv_acc = acc_pair
        q_cur = lax.dynamic_index_in_dim(q_blocks, blk_idx, axis=1, keepdims=False)
        do_cur = lax.dynamic_index_in_dim(do_blocks, blk_idx, axis=1, keepdims=False)
        delta_cur = lax.dynamic_index_in_dim(row_dot, blk_idx, axis=2, keepdims=False)
        lse_cur = lax.dynamic_index_in_dim(lse_blocks, blk_idx, axis=0, keepdims=False)
        scores = block_scores(q_cur, k_all, slopes, q_offset + blk_idx * q_blk, score_scale)
        prob_blk = jnp.exp(scores - lse_cur[..., None])
        dv_acc = dv_acc + jnp.einsum('bhqk,bqhd->bkhd', prob_blk.astype(jnp.bfloat16), do_cur, preferred_element_type=jnp.float32)
        d_probs = jnp.einsum('bqhd,bkhd->bhqk', do_cur, v_all, preferred_element_type=jnp.float32)
        d_scores = (prob_blk * (d_probs - delta_cur[..., None]) * score_scale).astype(jnp.bfloat16)
        dq_cur = jnp.einsum('bhqk,bkhd->bqhd', d_scores, k_all, preferred_element_type=jnp.float32)
        dk_acc = dk_acc + jnp.einsum('bhqk,bqhd->bkhd', d_scores, q_cur, preferred_element_type=jnp.float32)
        return (dk_acc, dv_acc), dq_cur.astype(jnp.bfloat16)

    zero_acc = jnp.zeros(k_all.shape, jnp.float32)
    acc_final, dq_blocks = lax.scan(one_block, (zero_acc, zero_acc), jnp.arange(n_blk))
    d_q = jnp.moveaxis(dq_blocks, 0, 1).reshape(n_batch, q_len, n_heads, head_dim)
    return d_q, acc_final[0], acc_final[1]


def solution(mesh):
    n_sp = mesh.shape['sp']
    seq_spec = P(None, 'sp', None)
    rep_spec = P()

    def local_step(x, ln1_w, w_qkv, q_ln_w, k_ln_w, w_out, grad_y):
        n_batch, tok_loc, d_model = x.shape
        n_heads, head_dim = q_ln_w.shape
        heads_loc = n_heads // n_sp
        seq_len = tok_loc * n_sp
        head_base = lax.axis_index('sp') * heads_loc
        slopes = lax.dynamic_slice_in_dim(alibi_slopes(n_heads), head_base, heads_loc)
        head_shape = (n_batch, tok_loc, n_heads, head_dim)
        flat_shape = (n_batch, tok_loc, d_model)
        x_f32 = x.astype(jnp.float32)
        h_f32, ln1_pull = jax.vjp(layer_norm, x_f32, ln1_w.astype(jnp.float32))
        h_act = h_f32.astype(jnp.bfloat16)
        qkv_raw = jnp.einsum('btd,de->bte', h_act, w_qkv, preferred_element_type=jnp.float32)
        q_f32, q_pull = jax.vjp(layer_norm, qkv_raw[..., :d_model], q_ln_w.reshape(d_model).astype(jnp.float32))
        k_f32, k_pull = jax.vjp(layer_norm, qkv_raw[..., d_model:2 * d_model], k_ln_w.reshape(d_model).astype(jnp.float32))
        qkv_tok = jnp.stack([q_f32.astype(jnp.bfloat16).reshape(head_shape), k_f32.astype(jnp.bfloat16).reshape(head_shape), qkv_raw[..., 2 * d_model:].astype(jnp.bfloat16).reshape(head_shape)])
        qkv_head = lax.all_to_all(qkv_tok, 'sp', 3, 2, tiled=True)
        q_blk = math.gcd(seq_len, 256)
        o_head, lse_blocks = attn_forward(qkv_head[0], qkv_head[1], qkv_head[2], slopes, 0, q_blk)
        o_tok = lax.all_to_all(o_head, 'sp', 1, 2, tiled=True).reshape(flat_shape)
        y = (jnp.einsum('btd,de->bte', o_tok, w_out, preferred_element_type=jnp.float32) + x_f32).astype(jnp.bfloat16)
        grad_w_out = jnp.einsum('btd,bte->de', o_tok, grad_y, preferred_element_type=jnp.float32)
        d_o = jnp.einsum('bte,de->btd', grad_y, w_out, preferred_element_type=jnp.float32).astype(jnp.bfloat16)
        d_o_head = lax.all_to_all(d_o.reshape(head_shape), 'sp', 2, 1, tiled=True)
        d_q, d_k, d_v = attn_backward(qkv_head[0], qkv_head[1], qkv_head[2], o_head, d_o_head, lse_blocks, slopes, 0, q_blk)
        d_qkv_head = jnp.stack([d_q, d_k.astype(jnp.bfloat16), d_v.astype(jnp.bfloat16)])
        d_qkv_tok = lax.all_to_all(d_qkv_head, 'sp', 2, 3, tiled=True)
        dq_raw, grad_q_ln = q_pull(d_qkv_tok[0].reshape(flat_shape).astype(jnp.float32))
        dk_raw, grad_k_ln = k_pull(d_qkv_tok[1].reshape(flat_shape).astype(jnp.float32))
        d_qkv = jnp.concatenate([dq_raw.astype(jnp.bfloat16), dk_raw.astype(jnp.bfloat16), d_qkv_tok[2].reshape(flat_shape)], axis=-1)
        grad_w_qkv = jnp.einsum('btd,bte->de', h_act, d_qkv, preferred_element_type=jnp.float32)
        d_h = jnp.einsum('bte,de->btd', d_qkv, w_qkv, preferred_element_type=jnp.float32).astype(jnp.bfloat16)
        d_x_norm, grad_ln1 = ln1_pull(d_h.astype(jnp.float32))
        grad_x = (d_x_norm + grad_y.astype(jnp.float32)).astype(jnp.bfloat16)
        weight_grads = lax.psum((grad_ln1, grad_w_qkv, grad_q_ln.reshape(n_heads, head_dim), grad_k_ln.reshape(n_heads, head_dim), grad_w_out), 'sp')
        return (y, grad_x) + tuple(weight_grads)

    return jax.shard_map(local_step, mesh=mesh, in_specs=(seq_spec, rep_spec, rep_spec, rep_spec, rep_spec, rep_spec, seq_spec), out_specs=(seq_spec, seq_spec, rep_spec, rep_spec, rep_spec, rep_spec, rep_spec), check_vma=False)
```

profile of v0, /device:TPU:0, one launch (start us, length us, event | category | flops | bytes accessed | tf_op | source)
XLA Modules:
  0.0 2828.3 jit_solution(11373139276411855591)
XLA Ops:
  51.2 37.9 %fusion.50 = f32[8,256,4608]{2,1,0:T(8,128)} fusion(bf16[1536,4608]{1,0:T(8,128)(2,1)} %param.13, bf16[8,256,1536]{2,1,0:T(8,128)(2,1)S(1)} %bitcast.176, f32[1536]{0:T(1024)S(1)} %convert_element_type.111, f32[8,256]{1,0:T(8,128)S(1)} %fusion.68, f32[8,256]{1,0:T(8,128)S(1)} %broadcast_multiply_fusion.4), kind=kOutput, calls=%fused_computation.72 | convolution fusion | flops 29006757888 | bytes 58218496 | tf_op jit(solution)/shard_map/btd,de->bte/dot_general | solution.py:99
  196.3 186.5 %all-to-all-done = bf16[3,8,256,16,96]{2,4,1,0,3:T(8,128)(2,1)} async-done(((bf16[3,8,256,16,96]{2,4,1,0,3:T(8,128)(2,1)}), bf16[3,8,256,16,96]{2,4,1,0,3:T(8,128)(2,1)}, u32[]{:S(2)}, u32[]{:S(2)}) %all-to-all-start) | async-done | bytes 18874400 | tf_op jit(solution)/shard_map/all_to_all | solution.py:103
  444.3 471.8 %while.27 = (s32[]{:T(128)}, bf16[8,8,256,2,96]{2,4,3,1,0:T(8,128)(2,1)}, f32[8,8,2,256]{3,2,1,0:T(2,128)S(1)}, s32[8]{0:T(128)S(1)}, bf16[8,8,256,2,96]{2,4,3,0...) while((s32[]{:T(128)}, ...), condition=%wide.region_9.10_spmd, body=%wide.region_6.9_spmd.sunk | while | flops 3342594304 | bytes 154799344 | solution.py:48
  958.2 792.6 %while.28 = (s32[]{:T(128)}, f32[8,2048,2,96]{1,3,2,0:T(8,128)}, f32[8,2048,2,96]{1,3,2,0:T(8,128)}, bf16[8,8,256,2,96]{2,4,3,1,0:T(8,128)(2,1)}, s32[8]{0:T(128...) while((s32[]{:T(128)}, f32[8,2048,2,96]{1,3,2,0:T(8,128)}, ...), condition=%wide.region_11.12_spmd.clone, body=%wide.region_10.11_spmd.clone.sunk | while | flops 8178237440 | bytes 242633984 | solution.py:77
  1001.3 26.1 multiply_convert_fusion.4
  1097.5 26.1 multiply_convert_fusion.4
  1175.2 22.1 bitcast_add_fusion.5
  1197.3 26.1 multiply_convert_fusion.4
  1274.9 22.1 bitcast_add_fusion.5
  1297.0 26.1 multiply_convert_fusion.4
  1374.7 22.1 bitcast_add_fusion.5
  1396.8 26.1 multiply_convert_fusion.4
  1474.5 22.1 bitcast_add_fusion.5
  1496.5 26.1 multiply_convert_fusion.4
  1574.2 22.1 bitcast_add_fusion.5
  1596.3 26.1 multiply_convert_fusion.4
  1696.1 26.1 multiply_convert_fusion.4
  1800.4 59.6 %copy.110 = bf16[3,8,2048,2,96]{4,3,1,0,2:T(2,128)(2,1)} copy(bf16[3,8,2048,2,96]{2,4,3,1,0:T(8,128)(2,1)} %pad_maximum_fusion.1) | data formatting | bytes 37748736 | tf_op jit(solution)/shard_map/stack | solution.py:112
  1900.9 238.2 %all-to-all-done.3 = bf16[3,8,2048,2,96]{4,3,1,0,2:T(2,128)(2,1)} async-done(((bf16[3,8,2048,2,96]{4,3,1,0,2:T(2,128)(2,1)}), bf16[3,8,2048,2,96]{4,3,1,0,2:T(2,128)(2,1)}, u32[]{:S(2)}, u32[]{:S(2)}) %all-to-all-start.3) | async-done | bytes 18874400 | tf_op jit(solution)/shard_map/all_to_all | solution.py:113
  2139.1 40.6 %copy.137 = bf16[3,8,8,256,2,96]{3,2,5,4,1,0:T(8,128)(2,1)} copy(bf16[3,8,8,256,2,96]{5,4,1,0,3,2:T(2,128)(2,1)} %bitcast.31) | data formatting | bytes 37748736 | tf_op jit(solution)/shard_map/all_to_all | solution.py:113
  2316.8 45.2 %convolution_bitcast_fusion = f32[1536,4608]{1,0:T(8,128)} fusion(bf16[8,256,1536]{2,1,0:T(8,128)(2,1)} %copy.117, bf16[8,256,1536]{2,1,0:T(8,128)(2,1)} %get-tuple-element.297, bf16[8,256,1536]{2,1,0:T(8,128)(2,1)} %get-tuple-element.296, bf16[8,256,1536]{2,1,0:T(8,128)(2,1)} %param.11, f32[1536]{0:T(1024)S(1)} %copy-done.17, f32[8,256]{1,0:T(8,128)S(1)} %copy-done.19, ...), kind=kOutput, calls=%fused_computation.52 | convolution fusion | flops 29063380992 | bytes 53499904 | tf_op jit(solution)/shard_map/btd,bte->de/dot_general | solution.py:117
  2378.5 38.7 %fusion.55 = (f32[8,256]{1,0:T(8,128)S(1)}, bf16[8,256,1536]{2,1,0:T(8,128)(2,1)}) fusion(bf16[8,256,1536]{2,1,0:T(8,128)(2,1)} %param.11, f32[1536]{0:T(1024)S(1)} %copy-done.17, f32[8,256]{1,0:T(8,128)S(1)} %copy-done.11, bf16[1536,4608]{1,0:T(8,128)(2,1)} %param.13, bf16[8,256,1536]{2,1,0:T(8,128)(2,1)} %copy.117, ...), kind=kOutput, calls=%fused_computation.77 | convolution fusion | flops 29069670400 | bytes 45635584 | tf_op jit(solution)/shard_map/bte,de->btd/dot_general | solution.py:118
  2426.1 23.6 all-reduce
  2460.8 334.7 %all-reduce.4.cloned.1.call-done = (f32[1536,4608]{1,0:T(8,128)}, f32[1536,1536]{1,0:T(8,128)}) async-done(((f32[1536,4608]{1,0:T(8,128)}, f32[1536,1536]{1,0:T(8,128)}), (f32[1536,4608]{1,0:T(8,128)}, f32[1536,1536]{1,0:T(8,128)})) %all-reduce.4.cloned.1.call-update) | async-done | bytes 37748752 | tf_op jit(solution)/shard_map/psum | solution.py:121
  (340 shorter events, 1446.5 us)
Async XLA Ops:
  37.0 134.5 %all-to-all-start.2 = ((bf16[8,256,16,96]{1,3,0,2:T(8,128)(2,1)}), bf16[8,256,16,96]{1,3,0,2:T(8,128)(2,1)}, u32[]{:S(2)}, u32[]{:S(2)}) async-start(bf16[8,256,16,96]{1,3,0,2:T(8,128)(2,1)} %copy.103), calls=%async_computation.2 | async-start | bytes 12582912 | tf_op jit(solution)/shard_map/all_to_all | solution.py:110
  51.2 37.9 %copy-start.27 = (bf16[16,96]{1,0:T(8,128)(2,1)S(1)}, bf16[16,96]{1,0:T(8,128)(2,1)}, u32[]{:S(2)}) copy-start(bf16[16,96]{1,0:T(8,128)(2,1)} %param.14) | copy-start | bytes 9220
  51.2 38.0 %copy-start.28 = (bf16[16,96]{1,0:T(8,128)(2,1)S(1)}, bf16[16,96]{1,0:T(8,128)(2,1)}, u32[]{:S(2)}) copy-start(bf16[16,96]{1,0:T(8,128)(2,1)} %param.15) | copy-start | bytes 9220
  89.2 36.0 %copy-start.8 = (f32[1536]{0:T(1024)}, f32[1536]{0:T(1024)S(1)}, u32[]{:S(2)}) copy-start(f32[1536]{0:T(1024)S(1)} %reshape.231) | copy-start | bytes 18436
  89.3 35.9 %copy-start.6 = (f32[1536]{0:T(1024)}, f32[1536]{0:T(1024)S(1)}, u32[]{:S(2)}) copy-start(f32[1536]{0:T(1024)S(1)} %reshape.232) | copy-start | bytes 18436
  171.4 211.4 %all-to-all-start = ((bf16[3,8,256,16,96]{2,4,1,0,3:T(8,128)(2,1)}), bf16[3,8,256,16,96]{2,4,1,0,3:T(8,128)(2,1)}, u32[]{:S(2)}, u32[]{:S(2)}) async-start(bf16[3,8,256,16,96]{2,4,1,0,3:T(8,128)(2,1)} %copy.92), calls=%async_computation | async-start | bytes 37748736 | tf_op jit(solution)/shard_map/all_to_all | solution.py:103
  468.1 17.9 copy-start
  527.1 17.9 copy-start
  586.1 17.9 copy-start
  645.1 17.9 copy-start
  704.0 17.9 copy-start
  763.0 17.9 copy-start
  822.0 17.9 copy-start
  881.0 17.9 copy-start
  950.9 909.1 %all-to-all-start.1 = ((bf16[8,2048,2,96]{3,2,0,1:T(2,128)(2,1)}), bf16[8,2048,2,96]{3,2,0,1:T(2,128)(2,1)}, u32[]{:S(2)}, u32[]{:S(2)}) async-start(bf16[8,2048,2,96]{3,2,0,1:T(2,128)(2,1)} %copy.98), calls=%async_computation.1 | async-start | bytes 16777216 | tf_op jit(solution)/shard_map/all_to_all | solution.py:106
  1860.0 279.1 %all-to-all-start.3 = ((bf16[3,8,2048,2,96]{4,3,1,0,2:T(2,128)(2,1)}), bf16[3,8,2048,2,96]{4,3,1,0,2:T(2,128)(2,1)}, u32[]{:S(2)}, u32[]{:S(2)}) async-start(bf16[3,8,2048,2,96]{4,3,1,0,2:T(2,128)(2,1)} %copy.110), calls=%async_computation.3 | async-start | bytes 50331648 | tf_op jit(solution)/shard_map/all_to_all | solution.py:113
  1865.2 930.3 %all-reduce.4.cloned.1.call-start = ((), (), s32[]{:S(2)}) async-start(), calls=%async_computation.4 | async-start | bytes 75497472 | tf_op jit(solution)/shard_map/psum | solution.py:121
  2263.1 27.3 slice-start
  2272.9 17.9 slice-start.2
  2298.6 18.1 copy-start.11
  2298.6 18.1 copy-start.17
  2298.6 18.1 copy-start.19
  2378.5 38.7 %copy-start.21 = (f32[8,256]{1,0:T(8,128)S(1)}, f32[8,256]{1,0:T(8,128)}, u32[]{:S(2)}) copy-start(f32[8,256]{1,0:T(8,128)} %copy-done.20) | copy-start | bytes 24580
  2795.5 22.0 copy-start.1
  (26 other events, 255.0 us)
Sparse Core Ops, SparseCore 0:
  2362.2 433.2 all-reduce.3
where the time goes:
time: 2840 us; the launch traced here: 2830 us
  matrix products  1200 us (42%)
  waiting for transfers between devices  759 us (27%)
  local copies, waits for them, and re-layouts  414 us (15%)
  other arithmetic  353 us (12%)
  loops' own time  42.9 us (2%)
    psum x1, waiting for transfers between devices, local_step(): lax.psum((grad_ln1, grad_w_qkv, grad_q_ln.reshape(n_heads, head_dim), gra...  335 us
    dot_general x16, matrix products, block_scores(): jnp.einsum('bqhd,bkhd->bhqk', q_cur, k_all, preferred_element_type=jnp.fl...  289 us
    all_to_all x1, waiting for transfers between devices, local_step(): d_qkv_tok = lax.all_to_all(d_qkv_head, 'sp', 2, 3, tiled=True)  238 us
    dot_general x8, matrix products, one_block(): jnp.einsum('bqhd,bkhd->bhqk', do_cur, v_all, preferred_element_type=jnp.f...  209 us
    all_to_all x1, waiting for transfers between devices, local_step(): qkv_head = lax.all_to_all(qkv_tok, 'sp', 3, 2, tiled=True)  186 us
    dot_general x8, matrix products, one_block(): jnp.einsum('bhqk,bqhd->bkhd', prob_blk.astype(jnp.bfloat16), do_cur, pref...  174 us
    reduce_sum x8, other arithmetic, one_block(): row_sum = jnp.sum(weights, axis=-1)  143 us
    dot_general x8, matrix products, one_block(): jnp.einsum('bhqk,bkhd->bqhd', weights.astype(jnp.bfloat16), v_all, prefer...  137 us
  transfers between devices with their start and end apart: 5, of which 3 were waited for; matrix products, arithmetic and copies ran while one was open for 40% of the time, Pallas kernels for 0%

commit v1 on v0

v1 whole, which is shorter than its diff:
```python
import math
import jax
import jax.numpy as jnp
import numpy as np
from jax import lax
from jax.experimental import pallas as pl
from jax.experimental.pallas import tpu as pltpu
from jax.sharding import PartitionSpec as P

F32 = jnp.float32
BF16 = jnp.bfloat16
LOG2E = 1.4426950408889634
PAD = 128
BLK = 512
CHUNKS = 4
SUM_STEPS = {0: [(0, ch) for ch in range(4)], 1: [(1, ch) for ch in range(4)], 4: [(2, 0)], 6: [(2, 1)], 7: [(2, 2)], 8: [(3, 0)],
             9: [(2, 3), (3, 1)], 10: [(4, 0)], 11: [(3, 2), (4, 1)], 12: [(3, 3)], 13: [(4, 2)], 14: [(4, 3)]}
BACK_STEPS = {0: [(0, ch) for ch in range(4)], 1: [(1, ch) for ch in range(4)], 3: [(2, 0)], 4: [(2, 1), (2, 2)], 5: [(2, 3), (3, 0)],
              6: [(3, 1), (3, 2), (4, 0)], 7: [(3, 3), (4, 1), (4, 2), (4, 3)]}
COLS = 512
TOK = 256


def alibi_slopes(n_heads):
    pow_two = 2 ** math.ceil(math.log2(n_heads))
    slopes = [2.0 ** (-8.0 * k / pow_two) for k in range(1, pow_two + 1)]
    if pow_two != n_heads:
        slopes = (slopes[1::2] + slopes[0::2])[:n_heads]
    return np.asarray(slopes, np.float64)


def slope_rows(n_heads, head_dim):
    raw = alibi_slopes(n_heads) * math.sqrt(head_dim)
    rows = np.zeros((n_heads, PAD - head_dim, 128), np.float32)
    rest = raw.copy()
    for part in range(3):
        cur = rest.astype(BF16).astype(np.float64)
        rows[:, part, :] = cur[:, None]
        rows[:, part + 3, :] = cur[:, None]
        rest = rest - cur
    return jnp.asarray(rows, BF16)


def key_bias_cols(seq_len, head_dim):
    pos = lax.broadcasted_iota(jnp.int32, (seq_len, PAD - head_dim), 0)
    col = lax.broadcasted_iota(jnp.int32, (seq_len, PAD - head_dim), 1)
    low = pos & 255
    val = jnp.where(col < 3, pos - low, jnp.where(col < 6, low, 0))
    return val.astype(F32).astype(BF16)


def causal_mask(values, fill):
    kpos = lax.broadcasted_iota(jnp.int32, values.shape, 0)
    qpos = lax.broadcasted_iota(jnp.int32, values.shape, 1)
    return jnp.where(kpos <= qpos, values, fill)


def fwd_kernel(q_ref, k_ref, v_ref, srow_ref, o_ref, lse_ref, k_sc, q_sc, s_sc):
    head_dim, seq_len = q_ref.shape
    coef = LOG2E / math.sqrt(head_dim)

    @pl.when(pl.program_id(0) == 0)
    def _():
        k_sc[:, head_dim:] = key_bias_cols(seq_len, head_dim)

    k_sc[:, :head_dim] = k_ref[...].T
    q_sc[:head_dim, :] = q_ref[...]
    for lane in range(0, seq_len, 128):
        q_sc[head_dim:, lane:lane + 128] = srow_ref[0]
    n_blk = seq_len // BLK
    for qb in range(n_blk):
        qs = slice(qb * BLK, (qb + 1) * BLK)
        buf = s_sc.at[qb % 2]
        row_max = None
        for kb in range(qb + 1):
            ks = slice(kb * BLK, (kb + 1) * BLK)
            raw = jnp.dot(k_sc[ks, :], q_sc[:, qs], preferred_element_type=F32)
            if kb == qb:
                raw = causal_mask(raw, -1e30)
            buf[ks, :] = raw
            cur = jnp.max(raw, axis=0, keepdims=True)
            row_max = cur if row_max is None else jnp.maximum(row_max, cur)
        shift = row_max * coef
        acc, row_sum = None, None
        for kb in range(qb + 1):
            ks = slice(kb * BLK, (kb + 1) * BLK)
            prob = jnp.exp2(buf[ks, :] * coef - shift)
            part = jnp.sum(prob, axis=0, keepdims=True)
            out = jnp.dot(v_ref[:, ks], prob.astype(BF16), preferred_element_type=F32)
            row_sum = part if row_sum is None else row_sum + part
            acc = out if acc is None else acc + out
        o_ref[:, qs] = (acc / row_sum).astype(BF16)
        lse_ref[0, :, qs] = shift + jnp.log2(row_sum)


def ride_along(g_ref, gsum_ref, sum_refs, steps, step):
    phases = sum_phases(g_ref, gsum_ref, *sum_refs)

    def advance(todo):
        for phase, ch in todo:
            phases[phase](ch)

    for at, todo in steps.items():
        @pl.when(step == at)
        def _():
            if at == 0:
                meet_all(lax.axis_index('sp'), lax.axis_size('sp'))
            advance(todo)
    return advance


def end_ride(advance, step):
    @pl.when(step == pl.num_programs(0) - 1)
    def _():
        advance([(phase, ch) for phase in (5, 6) for ch in range(CHUNKS)])


def bwd_kernel(q_ref, k_ref, v_ref, srow_ref, o_ref, do_ref, lse_ref, g_ref, dq_ref, dk_ref, dv_ref, gsum_ref,
               k_sc, q_sc, v_sc, qt_sc, dot_sc, p_sc, ds_sc, dq_sc, *sum_refs):
    step = pl.program_id(0)
    advance = ride_along(g_ref, gsum_ref, sum_refs, SUM_STEPS, step)
    head_dim, seq_len = q_ref.shape
    scale = head_dim ** -0.5
    coef = LOG2E * scale

    @pl.when(pl.program_id(0) == 0)
    def _():
        k_sc[:, head_dim:] = key_bias_cols(seq_len, head_dim)

    k_sc[:, :head_dim] = k_ref[...].T
    v_sc[...] = v_ref[...].T
    qt_sc[...] = q_ref[...].T
    dot_sc[...] = do_ref[...].T
    q_sc[:head_dim, :] = q_ref[...]
    for lane in range(0, seq_len, 128):
        q_sc[head_dim:, lane:lane + 128] = srow_ref[0]
    delta = jnp.sum(do_ref[...].astype(F32) * o_ref[...].astype(F32), axis=0, keepdims=True)
    lse = lse_ref[0]
    n_blk = seq_len // BLK
    for kb in range(n_blk):
        ks = slice(kb * BLK, (kb + 1) * BLK)
        for qb in range(kb, n_blk):
            qs = slice(qb * BLK, (qb + 1) * BLK)
            raw = jnp.dot(k_sc[ks, :], q_sc[:, qs], preferred_element_type=F32)
            prob = jnp.exp2(raw * coef - lse[:, qs])
            if qb == kb:
                prob = causal_mask(prob, 0.0)
            d_prob = jnp.dot(v_sc[ks, :], do_ref[:, qs], preferred_element_type=F32)
            d_s = (prob * (d_prob - delta[:, qs])).astype(BF16)
            p_sc[:, qs] = prob.astype(BF16)
            ds_sc[:, qs] = d_s
            d_q = jnp.dot(k_ref[:, ks], d_s, preferred_element_type=F32)
            if kb == 0:
                dq_sc[:, qs] = d_q
            else:
                dq_sc[:, qs] += d_q
        rest = slice(kb * BLK, seq_len)
        d_v = jnp.dot(p_sc[:, rest], dot_sc[rest, :], preferred_element_type=F32)
        d_k = jnp.dot(ds_sc[:, rest], qt_sc[rest, :], preferred_element_type=F32)
        dv_ref[:, ks] = d_v.T.astype(BF16)
        dk_ref[:, ks] = (d_k * scale).T.astype(BF16)
    dq_ref[...] = (dq_sc[...] * scale).astype(BF16)

    end_ride(advance, step)


def head_spec(head_dim, seq_len):
    return pl.BlockSpec((head_dim, seq_len), lambda h: (h, 0))


def attention_fwd(q_t, k_t, v_t, srows, n_heads):
    width, seq_len = q_t.shape
    head_dim = width // n_heads
    spec = head_spec(head_dim, seq_len)
    pairs = seq_len * seq_len // 2 * n_heads
    return pl.pallas_call(
        fwd_kernel,
        grid=(n_heads,),
        in_specs=[spec, spec, spec, pl.BlockSpec((1,) + srows.shape[1:], lambda h: (h, 0, 0))],
        out_specs=[spec, pl.BlockSpec((1, 1, seq_len), lambda h: (h, 0, 0))],
        out_shape=[jax.ShapeDtypeStruct((width, seq_len), BF16), jax.ShapeDtypeStruct((n_heads, 1, seq_len), F32)],
        scratch_shapes=[pltpu.VMEM((seq_len, PAD), BF16), pltpu.VMEM((PAD, seq_len), BF16), pltpu.VMEM((2, seq_len, BLK), F32)],
        compiler_params=pltpu.CompilerParams(dimension_semantics=('arbitrary',), vmem_limit_bytes=60 * 2 ** 20),
        cost_estimate=pl.CostEstimate(flops=pairs * 4 * 256, bytes_accessed=width * seq_len * 8, transcendentals=pairs),
        name='attn_fwd',
    )(q_t, k_t, v_t, srows)


def attention_bwd(q_t, k_t, v_t, srows, o_t, do_t, lse, n_heads, gwo):
    width, seq_len = q_t.shape
    head_dim = width // n_heads
    spec = head_spec(head_dim, seq_len)
    pairs = seq_len * seq_len // 2 * n_heads
    grad_shape = jax.ShapeDtypeStruct((width, seq_len), BF16)
    return pl.pallas_call(
        bwd_kernel,
        grid=(n_heads,),
        in_specs=[spec, spec, spec, pl.BlockSpec((1,) + srows.shape[1:], lambda h: (h, 0, 0)), spec, spec,
                  pl.BlockSpec((1, 1, seq_len), lambda h: (h, 0, 0)), pl.BlockSpec(memory_space=pl.ANY)],
        out_specs=[spec, spec, spec, pl.BlockSpec(memory_space=pl.ANY)],
        out_shape=[grad_shape, grad_shape, grad_shape, jax.ShapeDtypeStruct(sum_shape(gwo), F32)],
        scratch_shapes=[pltpu.VMEM((seq_len, PAD), BF16), pltpu.VMEM((PAD, seq_len), BF16), pltpu.VMEM((seq_len, head_dim), BF16),
                        pltpu.VMEM((seq_len, head_dim), BF16), pltpu.VMEM((seq_len, head_dim), BF16),
                        pltpu.VMEM((BLK, seq_len), BF16), pltpu.VMEM((BLK, seq_len), BF16), pltpu.VMEM((head_dim, seq_len), F32)]
                       + sum_scratch(*gwo.shape),
        compiler_params=pltpu.CompilerParams(dimension_semantics=('arbitrary',), collective_id=1, has_side_effects=True, vmem_limit_bytes=60 * 2 ** 20),
        cost_estimate=pl.CostEstimate(flops=pairs * 10 * 256, bytes_accessed=width * seq_len * 16, transcendentals=pairs),
        name='attn_bwd',
    )(q_t, k_t, v_t, srows, o_t, do_t, lse, gwo.reshape(sum_shape(gwo)))


def row_stats(values, axis):
    centered = values - jnp.mean(values, axis=axis, keepdims=True)
    rstd = lax.rsqrt(jnp.mean(centered * centered, axis=axis, keepdims=True) + 1e-5)
    return centered * rstd, rstd


def norm_grad(cot, unit, rstd, weight, axis):
    scaled = cot * weight
    mean_a = jnp.mean(scaled, axis=axis, keepdims=True)
    mean_b = jnp.mean(scaled * unit, axis=axis, keepdims=True)
    return rstd * (scaled - mean_a - unit * mean_b)


def wide(col_ref, width):
    return jnp.concatenate([col_ref[...]] * (width // 128), axis=1)


def xor_index(a, b):
    return sum(lax.rem(a // bit + b // bit, 2) * bit for bit in (1, 2, 4))


def proj_kernel(x_ref, ln1_ref, w_ref, qw_ref, kw_ref, ht_ref, q_ref, k_ref, v_ref, uq_ref, uk_ref, rq_ref, rk_ref, seq_ref,
                land, own_sem, send_sem, recv_sem):
    n_dev, _, d_model = land.shape
    step = pl.program_id(0)
    me = lax.axis_index('sp')

    def cp_block(hop):
        peer = xor_index(me, hop)
        return remote(x_ref.at[peer], land.at[hop], send_sem.at[hop], recv_sem.at[hop], peer)

    own = pltpu.make_async_copy(x_ref.at[me], land.at[0], own_sem)

    @pl.when(step == 0)
    def _():
        own.start()
        meet_all(me, n_dev)
        for hop in range(1, n_dev):
            cp_block(hop).start()
        own.wait()

    for hop in range(1, n_dev):
        @pl.when(step == hop)
        def _():
            cp_block(hop).wait()

    x_blk = land[step]
    seq_ref[...] = x_blk
    unit, _ = row_stats(x_blk.astype(F32), 1)
    h_act = (unit * ln1_ref[...]).astype(BF16)
    ht_ref[...] = h_act.T
    parts = ((0, q_ref, uq_ref, rq_ref, qw_ref), (d_model, k_ref, uk_ref, rk_ref, kw_ref))
    for base, out_ref, u_ref, r_ref, nw_ref in parts:
        raw = jnp.dot(h_act, w_ref[:, base:base + d_model], preferred_element_type=F32)
        unit, rstd = row_stats(raw, 1)
        unit = unit.T
        u_ref[...] = unit
        r_ref[...] = jnp.broadcast_to(rstd, (TOK, 128)).T[:1]
        out_ref[...] = (unit * wide(nw_ref, TOK)).astype(BF16)
    v_ref[...] = jnp.dot(h_act, w_ref[:, 2 * d_model:], preferred_element_type=F32).astype(BF16).T


def back_kernel(dq_ref, dk_ref, dv_ref, uq_ref, uk_ref, rq_ref, rk_ref, qw_ref, kw_ref, w_ref, x_ref, ln1_ref, gy_ref,
                g_ref, drq_ref, drk_ref, gx_ref, gqw_ref, gkw_ref, g1_ref, gsum_ref, d_sc, *sum_refs):
    d_model = x_ref.shape[1]
    step = pl.program_id(0)
    advance = ride_along(g_ref, gsum_ref, sum_refs, BACK_STEPS, step)

    @pl.when(step == 0)
    def _():
        gqw_ref[...] = jnp.zeros_like(gqw_ref)
        gkw_ref[...] = jnp.zeros_like(gkw_ref)
        g1_ref[...] = jnp.zeros_like(g1_ref)

    d_sc[2 * d_model:, :] = dv_ref[...]
    parts = ((0, dq_ref, uq_ref, rq_ref, qw_ref, drq_ref, gqw_ref), (d_model, dk_ref, uk_ref, rk_ref, kw_ref, drk_ref, gkw_ref))
    for base, d_ref, u_ref, r_ref, nw_ref, out_ref, gw_ref in parts:
        cot, unit = d_ref[...].astype(F32), u_ref[...]
        prod = cot * unit
        fold = prod[:, :128]
        for lane in range(128, TOK, 128):
            fold = fold + prod[:, lane:lane + 128]
        gw_ref[...] += fold
        d_raw = norm_grad(cot, unit, r_ref[...], wide(nw_ref, TOK), 0).astype(BF16)
        out_ref[...] = d_raw
        d_sc[base:base + d_model, :] = d_raw
    d_h = jnp.dot(w_ref[...], d_sc[...], preferred_element_type=F32)
    cot = d_h.astype(BF16).T.astype(F32)
    unit, rstd = row_stats(x_ref[...].astype(F32), 1)
    g1_ref[...] += jnp.sum(cot * unit, axis=0, keepdims=True)
    gx_ref[...] = (norm_grad(cot, unit, rstd, ln1_ref[...], 1) + gy_ref[...].astype(F32)).astype(BF16)
    end_ride(advance, step)


def token_specs(d_model):
    col = pl.BlockSpec((d_model, TOK), lambda t: (0, t))
    row = pl.BlockSpec((TOK, d_model), lambda t: (t, 0))
    stat = pl.BlockSpec((1, TOK), lambda t: (0, t))
    return col, row, stat


def whole(shape):
    return pl.BlockSpec(shape, lambda t: (0, 0), pipeline_mode=pl.Buffered(1))


def project(x, ln1_row, w_qkv, qw_col, kw_col):
    n_dev, _, d_model = x.shape
    seq_len = n_dev * TOK
    at = lambda t: xor_index(lax.axis_index('sp'), t)
    col = pl.BlockSpec((d_model, TOK), lambda t: (0, at(t)))
    stat = pl.BlockSpec((1, TOK), lambda t: (0, at(t)))
    act = jax.ShapeDtypeStruct((d_model, seq_len), BF16)
    act_f32 = jax.ShapeDtypeStruct((d_model, seq_len), F32)
    stat_f32 = jax.ShapeDtypeStruct((1, seq_len), F32)
    dma = pltpu.SemaphoreType.DMA
    return pl.pallas_call(
        proj_kernel,
        grid=(n_dev,),
        in_specs=[pl.BlockSpec(memory_space=pl.ANY), whole(ln1_row.shape), whole(w_qkv.shape), whole(qw_col.shape), whole(kw_col.shape)],
        out_specs=[col, col, col, col, col, col, stat, stat, pl.BlockSpec((TOK, d_model), lambda t: (at(t), 0))],
        out_shape=[act, act, act, act, act_f32, act_f32, stat_f32, stat_f32, jax.ShapeDtypeStruct((seq_len, d_model), BF16)],
        scratch_shapes=[pltpu.VMEM((n_dev, TOK, d_model), BF16), dma, dma((n_dev,)), dma((n_dev,))],
        compiler_params=pltpu.CompilerParams(dimension_semantics=('arbitrary',), collective_id=2, has_side_effects=True, vmem_limit_bytes=60 * 2 ** 20),
        cost_estimate=pl.CostEstimate(flops=6 * seq_len * d_model * d_model, bytes_accessed=40 * seq_len * d_model, transcendentals=0),
        name='project',
    )(x, ln1_row, w_qkv, qw_col, kw_col)


def back_project(dq_t, dk_t, dv_t, saved, qw_col, kw_col, w_qkv, x_seq, ln1_row, gy_seq, gwv):
    seq_len, d_model = x_seq.shape
    col, row, stat = token_specs(d_model)
    act = jax.ShapeDtypeStruct((d_model, seq_len), BF16)
    acc_spec = lambda shape: pl.BlockSpec(shape, lambda t: (0, 0), pipeline_mode=pl.Buffered(1))
    uq, uk, rq, rk = saved
    return pl.pallas_call(
        back_kernel,
        grid=(seq_len // TOK,),
        in_specs=[col, col, col, col, col, stat, stat, whole(qw_col.shape), whole(kw_col.shape), whole(w_qkv.shape), row, whole(ln1_row.shape), row, pl.BlockSpec(memory_space=pl.ANY)],
        out_specs=[col, col, row, acc_spec((d_model, 128)), acc_spec((d_model, 128)), acc_spec((1, d_model)), pl.BlockSpec(memory_space=pl.ANY)],
        out_shape=[act, act, jax.ShapeDtypeStruct((seq_len, d_model), BF16), jax.ShapeDtypeStruct((d_model, 128), F32),
                   jax.ShapeDtypeStruct((d_model, 128), F32), jax.ShapeDtypeStruct((1, d_model), F32), jax.ShapeDtypeStruct(sum_shape(gwv), F32)],
        scratch_shapes=[pltpu.VMEM((3 * d_model, TOK), BF16)] + sum_scratch(*gwv.shape),
        compiler_params=pltpu.CompilerParams(dimension_semantics=('arbitrary',), collective_id=3, has_side_effects=True, vmem_limit_bytes=67043328),
        cost_estimate=pl.CostEstimate(flops=6 * seq_len * d_model * d_model, bytes_accessed=40 * seq_len * d_model, transcendentals=0),
        name='back_project',
    )(dq_t, dk_t, dv_t, uq, uk, rq, rk, qw_col, kw_col, w_qkv, x_seq, ln1_row, gy_seq, gwv.reshape(sum_shape(gwv)))


def grad_kernel(*refs):
    h_ref, d_refs, out_ref = refs[0], refs[1:-1], refs[-1]
    steps = pl.num_programs(0) // len(d_refs)
    for part, d_ref in enumerate(d_refs):
        @pl.when(pl.program_id(0) // steps == part)
        def _():
            out_ref[...] = lax.dot_general(h_ref[...], d_ref[...], (((1,), (1,)), ((), ())), preferred_element_type=F32)


def weight_grad(h_t, parts):
    d_model, seq_len = h_t.shape
    steps = d_model // COLS
    col_map = lambda part: lambda i: (jnp.clip(i - part * steps, 0, steps - 1), 0)
    n_parts = len(parts)
    return pl.pallas_call(
        grad_kernel,
        grid=(n_parts * steps,),
        in_specs=[whole((d_model, seq_len))] + [pl.BlockSpec((COLS, seq_len), col_map(i)) for i in range(n_parts)],
        out_specs=pl.BlockSpec((d_model, COLS), lambda i: (0, i)),
        out_shape=jax.ShapeDtypeStruct((d_model, n_parts * d_model), F32),
        compiler_params=pltpu.CompilerParams(dimension_semantics=('arbitrary',), vmem_limit_bytes=60 * 2 ** 20),
        cost_estimate=pl.CostEstimate(flops=2 * n_parts * seq_len * d_model * d_model, bytes_accessed=8 * n_parts * d_model * d_model, transcendentals=0),
    )(h_t, *parts)


def sum_phases(g_ref, out_ref, acc, r0, r1, r2, loc_sem, p0_send, p0_recv, p1_send, p1_recv, p2_send, p2_recv,
               a2_send, a2_recv, a1_send, a1_recv, b1_send, b1_recv, ol_sem, or_send, or_recv):
    cols = acc.shape[-1]
    me = lax.axis_index('sp')
    core = lax.rem(me, 2)
    xb = lax.rem(me // 2, 2)
    yb = me // 4
    core_peer = me + 1 - 2 * core
    x_peer = me + 2 - 4 * xb
    y_peer = me + 4 - 8 * yb
    first, second = (xb, yb), (yb, xb)
    peer1, peer2 = (x_peer, y_peer), (y_peer, x_peer)

    def g1(ch, part):
        return r0.at[ch, part, 0]

    def g2(ch, part):
        return r0.at[ch, part, 1, 0]

    def span(ch):
        return pl.ds(pl.multiple_of(ch * cols, cols), cols)

    def cp_load(ch):
        return pltpu.make_async_copy(g_ref.at[core, :, :, :, :, span(ch)], acc.at[ch], loc_sem.at[ch])

    def cp_core(ch):
        return remote(g_ref.at[1 - core, :, :, :, :, span(ch)], r0.at[ch], p0_send.at[ch], p0_recv.at[ch], core_peer)

    def cp_first(ch, part):
        return remote(acc.at[ch, part, 1 - first[part]], r1.at[ch, part], p1_send.at[ch, part], p1_recv.at[ch, part], peer1[part])

    def cp_second(ch, part):
        return remote(r1.at[ch, part, 1 - second[part]], r2.at[ch, part], p2_send.at[ch, part], p2_recv.at[ch, part], peer2[part])

    def cp_back2(ch, part):
        return remote(r2.at[ch, part], g2(ch, part), a2_send.at[ch, part], a2_recv.at[ch, part], peer2[part])

    def cp_back1(ch, part):
        return remote(r2.at[ch, part], g1(ch, part).at[second[part]], a1_send.at[ch, part], a1_recv.at[ch, part], peer1[part])

    def cp_relay(ch, part):
        return remote(g2(ch, part), g1(ch, part).at[1 - second[part]], b1_send.at[ch, part], b1_recv.at[ch, part], peer1[part])

    def out_pair(ch, part, kind):
        if kind == 0:
            src, dst = r2.at[ch, part], out_ref.at[core, part, first[part], second[part], :, span(ch)]
        elif kind == 1:
            src, dst = g2(ch, part), out_ref.at[core, part, first[part], 1 - second[part], :, span(ch)]
        else:
            src, dst = g1(ch, part), out_ref.at[core, part, 1 - first[part], :, :, span(ch)]
        local = pltpu.make_async_copy(src, dst, ol_sem.at[ch, kind, part])
        return local, remote(src, dst, or_send.at[ch, kind, part], or_recv.at[ch, kind, part], core_peer)

    def start_out(ch, part, kind):
        for copy in out_pair(ch, part, kind):
            copy.start()

    def phase0(ch):
        cp_core(ch).start()
        cp_load(ch).start()

    def phase1(ch):
        cp_load(ch).wait()
        cp_core(ch).wait_recv()
        for part in range(2):
            for f in range(2):
                for s in range(2):
                    acc[ch, part, f, s] += r0[ch, part, f, s]
            cp_first(ch, part).start()

    def phase2(ch):
        for part in range(2):
            cp_first(ch, part).wait_recv()
            for s in range(2):
                r1[ch, part, s] += acc[ch, part, first[part], s]
            cp_second(ch, part).start()

    def phase3(ch):
        for part in range(2):
            cp_second(ch, part).wait_recv()
            r2[ch, part] += r1[ch, part, second[part]]
            cp_back2(ch, part).start()
            cp_back1(ch, part).start()
            start_out(ch, part, 0)

    def phase4(ch):
        for part in range(2):
            cp_back2(ch, part).wait_recv()
            cp_relay(ch, part).start()
            start_out(ch, part, 1)

    def phase5(ch):
        for part in range(2):
            cp_back1(ch, part).wait_recv()
            cp_relay(ch, part).wait_recv()
            start_out(ch, part, 2)

    def finish(ch):
        cp_core(ch).wait_send()
        for part in range(2):
            for make in (cp_first, cp_second, cp_back2, cp_back1, cp_relay):
                make(ch, part).wait_send()
            for kind in range(3):
                local, away = out_pair(ch, part, kind)
                local.wait()
                away.wait_send()
                away.wait_recv()

    return phase0, phase1, phase2, phase3, phase4, phase5, finish


def sum_scratch(rows, width):
    piece, cols = rows // 16, width // CHUNKS
    dma = pltpu.SemaphoreType.DMA
    buf = lambda *lead: pltpu.VMEM((CHUNKS,) + lead + (piece, cols), F32)
    return ([buf(2, 2, 2), buf(2, 2, 2), buf(2, 2), buf(2)] + [dma((CHUNKS,))] * 3 + [dma((CHUNKS, 2))] * 10
            + [dma((CHUNKS, 3, 2))] * 3)


def remote(src, dst, send, recv, peer):
    return pltpu.make_async_remote_copy(src_ref=src, dst_ref=dst, send_sem=send, recv_sem=recv, device_id=(peer,), device_id_type=pl.DeviceIdType.MESH)


def meet_all(me, n_dev):
    barrier = pltpu.get_barrier_semaphore()
    for hop in range(1, n_dev):
        pl.semaphore_signal(barrier, inc=1, device_id=(lax.rem(me + hop, n_dev),), device_id_type=pl.DeviceIdType.MESH)
    pl.semaphore_wait(barrier, n_dev - 1)


def reduce_kernel(g_ref, e_ref, out_ref, esum_ref, e_buf, e_send, e_recv, *sum_refs):
    me = lax.axis_index('sp')
    n_dev = e_buf.shape[0]
    meet_all(me, n_dev)
    phases = sum_phases(g_ref, out_ref, *sum_refs)

    def cp_small(hop, origin):
        return remote(e_ref, e_buf.at[origin], e_send.at[hop], e_recv.at[hop], lax.rem(me + hop, n_dev))

    for hop in range(1, n_dev):
        cp_small(hop, me).start()
    e_buf[me] = e_ref[...]
    for phase in phases:
        lax.fori_loop(0, CHUNKS, lambda ch, _: phase(ch), None)
    for hop in range(1, n_dev):
        cp_small(hop, lax.rem(me + n_dev - hop, n_dev)).wait()
    total = e_buf[0]
    for origin in range(1, n_dev):
        total = total + e_buf[origin]
    esum_ref[...] = total


def sum_shape(value):
    rows, width = value.shape
    return (2, 2, 2, 2, rows // 16, width)


def reduce_sum(value, small, n_dev):
    shape = sum_shape(value)
    dma = pltpu.SemaphoreType.DMA
    vmem = pl.BlockSpec(memory_space=pltpu.VMEM)
    out, small_sum = pl.pallas_call(
        reduce_kernel,
        in_specs=[pl.BlockSpec(memory_space=pl.ANY), vmem],
        out_specs=[pl.BlockSpec(memory_space=pl.ANY), vmem],
        out_shape=[jax.ShapeDtypeStruct(shape, F32), jax.ShapeDtypeStruct(small.shape, F32)],
        scratch_shapes=[pltpu.VMEM((n_dev,) + small.shape, F32), dma((n_dev,)), dma((n_dev,))] + sum_scratch(*value.shape),
        compiler_params=pltpu.CompilerParams(collective_id=0, has_side_effects=True, vmem_limit_bytes=60 * 2 ** 20),
        cost_estimate=pl.CostEstimate(flops=10 ** 9, bytes_accessed=8 * value.size, transcendentals=0),
        name='reduce_sum',
    )(value.reshape(shape), small)
    return out.reshape(value.shape), small_sum


def place_kernel(*refs):
    refs[-1][...] = refs[-2][...]


def place_columns(value, width, first, into=None):
    rows, cols = value.shape
    unit = min(cols, rows)
    step = rows // 6 if rows % 6 == 0 else rows // 4
    prior = [] if into is None else [into]
    return pl.pallas_call(
        place_kernel,
        grid=(rows // step, cols // unit),
        in_specs=[pl.BlockSpec(memory_space=pl.ANY)] * len(prior) + [pl.BlockSpec((step, unit), lambda i, j: (i, j))],
        out_specs=pl.BlockSpec((step, unit), lambda i, j: (i, j + first)),
        out_shape=jax.ShapeDtypeStruct((rows, width), value.dtype),
        input_output_aliases={0: 0} if prior else {},
        compiler_params=pltpu.CompilerParams(dimension_semantics=('arbitrary', 'arbitrary')),
        cost_estimate=pl.CostEstimate(flops=rows * cols, bytes_accessed=2 * rows * cols * value.dtype.itemsize, transcendentals=0),
        name='place_columns',
    )(*prior, value)


def dot(a, b, ca, cb):
    return lax.dot_general(a, b, (((ca,), (cb,)), ((), ())), preferred_element_type=F32)


def solution(mesh):
    seq_spec = P(None, 'sp', None)
    rep_spec = P()
    n_sp = mesh.shape['sp']

    def exchange(blocks):
        return lax.all_to_all(blocks, 'sp', 0, 0, tiled=True)

    def local_step(x, ln1_w, w_qkv, q_ln_w, k_ln_w, w_out, grad_y):
        n_batch, tok_loc, d_model = x.shape
        n_heads, head_dim = q_ln_w.shape
        seq_len = n_batch * tok_loc
        srows = slope_rows(n_heads, head_dim)
        ln1_row = ln1_w.astype(F32)[None]
        qw_col = jnp.broadcast_to(q_ln_w.reshape(d_model, 1).astype(F32), (d_model, 128))
        kw_col = jnp.broadcast_to(k_ln_w.reshape(d_model, 1).astype(F32), (d_model, 128))
        h_t, q_t, k_t, v_t, *saved, x_seq = project(x, ln1_row, w_qkv, qw_col, kw_col)
        x_seq, grad_y = lax.optimization_barrier((x_seq, grad_y))
        gy_seq = exchange(grad_y).reshape(seq_len, d_model)
        o_t, lse = attention_fwd(q_t, k_t, v_t, srows, n_heads)
        y_seq = (dot(o_t, w_out, 0, 0) + x_seq.astype(F32)).astype(BF16)
        y_seq, gy_seq = lax.optimization_barrier((y_seq, gy_seq))
        y = exchange(y_seq.reshape(x.shape))
        gwo_loc = dot(o_t, gy_seq, 1, 0)
        do_t = dot(w_out, gy_seq, 1, 1).astype(BF16)
        gwo_loc, do_t = lax.optimization_barrier((gwo_loc, do_t))
        dq_t, dk_t, dv_t, gwo_sum = attention_bwd(q_t, k_t, v_t, srows, o_t, do_t, lse, n_heads, gwo_loc)
        grad_w_out = gwo_sum.reshape(w_out.shape)
        gwv_loc = weight_grad(h_t, [dv_t])
        drq, drk, gx_seq, gqw, gkw, g1, gwv_sum = back_project(dq_t, dk_t, dv_t, saved, qw_col, kw_col, w_qkv, x_seq, ln1_row, gy_seq, gwv_loc)
        grad_w_v = gwv_sum.reshape(w_out.shape)
        y, gx_seq = lax.optimization_barrier((y, gx_seq))
        grad_x = exchange(gx_seq.reshape(x.shape))
        gwqk_loc = weight_grad(h_t, [drq, drk])
        y = place_columns(y.reshape(seq_len, d_model), d_model, 0).reshape(x.shape)
        grad_w_out = place_columns(grad_w_out, d_model, 0)
        partial = place_columns(grad_w_v, 3 * d_model, 2)
        small_loc = jnp.concatenate([g1, jnp.sum(gqw, axis=1)[None], jnp.sum(gkw, axis=1)[None], jnp.zeros((5, d_model), F32)], axis=0)
        y, grad_w_out, partial, gwqk_loc = lax.optimization_barrier((y, grad_w_out, partial, gwqk_loc))
        grad_w_qk, small = reduce_sum(gwqk_loc, small_loc, n_sp)
        grad_w_qkv = place_columns(grad_w_qk, 3 * d_model, 0, partial)
        return y, grad_x, small[0], grad_w_qkv, small[1].reshape(n_heads, head_dim), small[2].reshape(n_heads, head_dim), grad_w_out

    return jax.shard_map(local_step, mesh=mesh, in_specs=(seq_spec, rep_spec, rep_spec, rep_spec, rep_spec, rep_spec, seq_spec), out_specs=(seq_spec, seq_spec, rep_spec, rep_spec, rep_spec, rep_spec, rep_spec), check_vma=False)
```

time: 2840 us -> 771 us (0.27)
  matrix products: 1200 us -> 45.8 us
  waiting for transfers between devices: 759 us -> 0.01 us
  Pallas kernels: 0 us -> 693 us
  local copies, waits for them, and re-layouts: 414 us -> 14 us
  other arithmetic: 353 us -> 1.24 us
  loops' own time: 42.9 us -> 0 us
    dot_general x62 -> x3, matrix products: 1200 us -> 45.8 us  [dot(): lax.dot_general(a, b, (((ca,), (cb,)), ((), ())), preferred_element_type=...]
    pallas_call x0 -> x11, Pallas kernels: none -> 693 us  [the longest x1 180 us: reduce_sum(): pl.pallas_call(reduce_kernel, in_specs=[pl.BlockSpec(memory_space=pl.ANY)...]
    all_to_all x4 -> x3, waiting for transfers between devices: 425 us -> 0.01 us  [exchange(): return lax.all_to_all(blocks, 'sp', 0, 0, tiled=True)]
    psum x1 -> x0, waiting for transfers between devices: 335 us -> none  [local_step(): lax.psum((grad_ln1, grad_w_qkv, grad_q_ln.reshape(n_heads, head_dim), gra...]
    reduce_sum x16 -> x2, other arithmetic: 214 us -> 0.55 us  [the longest x1 0.27 us: local_step(): jnp.sum(gqw, axis=1)[None]]
    another operation x6 -> x2, local copies, waits for them, and re-layouts: 92.8 us -> 1.34 us  [the longest x1 0.67 us: local_step(): small[1].reshape(n_heads, head_dim)]
    all_to_all x5 -> x0, local copies, waits for them, and re-layouts: 90.7 us -> none  [the longest x1 40.6 us: local_step(): d_qkv_tok = lax.all_to_all(d_qkv_head, 'sp', 2, 3, tiled=True)]
    convert_element_type x9 -> x2, local copies, waits for them, and re-layouts: 77.7 us -> 1.53 us  [the longest x1 0.76 us: local_step(): k_ln_w.reshape(d_model, 1).astype(F32)]
  transfers between devices with their start and end apart: 5 -> 3, of which waited for: 3 -> 0; matrix products, arithmetic and copies ran while one was open for 40% -> 3% of each run, Pallas kernels for 0% -> 79%
where the time goes in v1:
time: 771 us; the launch traced here: 766 us
  Pallas kernels  693 us (90%)
  matrix products  45.8 us (6%)
  local copies, waits for them, and re-layouts  14 us (2%)
  starting transfers between devices  11.4 us (1%)
    pallas_call x1, Pallas kernels, reduce_sum(): pl.pallas_call(reduce_kernel, in_specs=[pl.BlockSpec(memory_space=pl.ANY)...  180 us
    pallas_call x1, Pallas kernels, attention_bwd(): pl.pallas_call(bwd_kernel, grid=(n_heads,), in_specs=[spec, spec, spec, p...  180 us
    pallas_call x1, Pallas kernels, back_project(): pl.pallas_call(back_kernel, grid=(seq_len // TOK,), in_specs=[col, col, c...  101 us
    pallas_call x1, Pallas kernels, project(): pl.pallas_call(proj_kernel, grid=(n_dev,), in_specs=[pl.BlockSpec(memory_...  85.2 us
    pallas_call x1, Pallas kernels, attention_fwd(): pl.pallas_call(fwd_kernel, grid=(n_heads,), in_specs=[spec, spec, spec, p...  64.3 us
    dot_general x3, matrix products, dot(): lax.dot_general(a, b, (((ca,), (cb,)), ((), ())), preferred_element_type=...  45.8 us
    pallas_call x2, Pallas kernels, weight_grad(): pl.pallas_call(grad_kernel, grid=(n_parts * steps,), in_specs=[whole((d_m...  42.5 us
    pallas_call x4, Pallas kernels, place_columns(): pl.pallas_call(place_kernel, grid=(rows // step, cols // unit), in_specs=...  40 us
  transfers between devices with their start and end apart: 3, of which 0 were waited for; matrix products, arithmetic and copies ran while one was open for 3% of the time, Pallas kernels for 79%

profile of v1, /device:TPU:0, one launch (start us, length us, event | category | flops | bytes accessed | tf_op | source)
XLA Modules:
  0.0 766.3 jit_solution(12341098347849891683)
XLA Ops:
  0.6 1.3 reshape.78.ln1_ref
  1.9 0.8 reshape.79
  2.7 0.8 reshape.80
  3.4 1.2 broadcast_in_dim.26.qw_ref
  4.6 1.1 broadcast_in_dim.27.kw_ref
  5.7 85.2 %project.1 = (bf16[1536,2048]{1,0:T(8,128)(2,1)}, bf16[1536,2048]{1,0:T(8,128)(2,1)}, bf16[1536,2048]{1,0:T(8,128)(2,1)}, bf16[1536,2048]{1,0:T(8,128)(2,1)}, f3...) custom-call(bf16[8,256,1536]{2,1,0:T(8,128)(2,1)} %x_ref.1, ...), custom_call_target="tpu_custom_call" | custom-call | flops 28991029248 | bytes 125829120 | tf_op jit(solution)/shard_map/project/pallas_call | solution.py:327
  91.0 4.0 all-to-all-start
  95.0 64.3 %attn_fwd.1 = (bf16[1536,2048]{1,0:T(8,128)(2,1)}, f32[16,1,2048]{2,1,0:T(1,128)}) custom-call(bf16[1536,2048]{1,0:T(8,128)(2,1)} %get-tuple-element.43.q_ref, bf16[1536,2048]{1,0:T(8,128)(2,1)} %get-tuple-element.44.k_ref, bf16[1536,2048]{1,0:T(8,128)(2,1)} %get-tuple-element.45.v_ref, bf16[16,32,128]{2,1,0:T(8,128)(2,1)} %constant.1.clone.srow_ref), custom_call_target="tpu_custom_call" | custom-call | flops 34359738368 | bytes 25165824 | tf_op jit(solution)/shard_map/attn_fwd/pallas_call | solution.py:176
  159.3 16.2 %add_convert_fusion = bf16[2048,1536]{1,0:T(8,128)(2,1)} fusion(bf16[2048,1536]{1,0:T(8,128)(2,1)} %get-tuple-element.48.x_ref, bf16[1536,2048]{1,0:T(8,128)(2,1)} %get-tuple-element.46.o_ref, bf16[1536,1536]{1,0:T(8,128)(2,1)} %param.13), kind=kOutput, calls=%fused_computation | convolution fusion | flops 9673113600 | bytes 23592960 | tf_op jit(solution)/shard_map/dot_general | solution.py:582
  175.5 15.6 %fusion.1 = f32[1536,1536]{1,0:T(8,128)} fusion(bf16[1536,2048]{1,0:T(8,128)(2,1)} %get-tuple-element.46.o_ref, bf16[2048,1536]{1,0:T(8,128)(2,1)} %bitcast.gy_ref), kind=kOutput, calls=%fused_computation.7 | convolution fusion | flops 9663676416 | bytes 22020096 | tf_op jit(solution)/shard_map/dot_general | solution.py:582
  191.1 14.0 %fusion.do_ref = bf16[1536,2048]{1,0:T(8,128)(2,1)} fusion(bf16[2048,1536]{1,0:T(8,128)(2,1)} %bitcast.gy_ref, bf16[1536,1536]{1,0:T(8,128)(2,1)S(1)} %bitcast.27), kind=kOutput, calls=%fused_computation.2 | convolution fusion | flops 9666822144 | bytes 17301504 | tf_op jit(solution)/shard_map/dot_general | solution.py:582
  205.1 3.5 all-to-all-start.1
  208.6 179.8 %attn_bwd.1 = (bf16[1536,2048]{1,0:T(8,128)(2,1)}, bf16[1536,2048]{1,0:T(8,128)(2,1)}, bf16[1536,2048]{1,0:T(8,128)(2,1)}, f32[2,2,2,2,96,1536]{5,4,3,2,1,0:T(8,128)}) custom-call(bf16[1536,2048]{1,0:T(8,128)(2,1)} %get-tuple-element.43.q_ref, bf16[1536,2048]{1,0:T(8,128)(2,1)} %get-tuple-element.44.k_ref, bf16[1536,2048]{1,0:T(8,128)(2,1)} %get-tuple-element.45.v_ref, ...), custom_call_target="tpu_custom_call" | custom-call | flops 85899345920 | bytes 50331648 | tf_op jit(solution)/shard_map/attn_bwd/pallas_call | solution.py:195
  388.4 15.6 %shard_map.135 = f32[1536,1536]{1,0:T(8,128)} custom-call(bf16[1536,2048]{1,0:T(8,128)(2,1)} %get-tuple-element.62.refs_0_, bf16[1536,2048]{1,0:T(8,128)(2,1)} %get-tuple-element.57.refs_1_.dv_ref), custom_call_target="tpu_custom_call" | custom-call | flops 9663676416 | bytes 18874368 | tf_op jit(solution)/shard_map/pallas_call | solution.py:374
  404.0 100.9 %back_project.1 = (bf16[1536,2048]{1,0:T(8,128)(2,1)}, bf16[1536,2048]{1,0:T(8,128)(2,1)}, bf16[2048,1536]{1,0:T(8,128)(2,1)}, f32[1536,128]{1,0:T(8,128)}, f32[...) custom-call(bf16[1536,2048]{1,0:T(8,128)(2,1)} %get-tuple-element.55.dq_ref, ...), custom_call_target="tpu_custom_call" | custom-call | flops 28991029248 | bytes 125829120 | tf_op jit(solution)/shard_map/back_project/pallas_call | solution.py:346
  504.9 3.9 all-to-all-start.2
  509.5 8.6 %place_columns.5 = f32[1536,1536]{1,0:T(8,128)} custom-call(f32[1536,1536]{1,0:T(8,128)} %bitcast.21), custom_call_target="tpu_custom_call" | custom-call | flops 2359296 | bytes 18874368 | tf_op jit(solution)/shard_map/place_columns/pallas_call | solution.py:568
  518.1 8.6 %place_columns.6.refs_0_ = f32[1536,4608]{1,0:T(8,128)} custom-call(f32[1536,1536]{1,0:T(8,128)} %bitcast.22), custom_call_target="tpu_custom_call" | custom-call | flops 2359296 | bytes 18874368 | tf_op jit(solution)/shard_map/place_columns/pallas_call | solution.py:568
  527.5 26.9 %shard_map.136 = f32[1536,3072]{1,0:T(8,128)} custom-call(bf16[1536,2048]{1,0:T(8,128)(2,1)} %get-tuple-element.62.refs_0_, bf16[1536,2048]{1,0:T(8,128)(2,1)} %get-tuple-element.67.refs_1_, bf16[1536,2048]{1,0:T(8,128)(2,1)} %get-tuple-element.68.refs_2_), custom_call_target="tpu_custom_call" | custom-call | flops 19327352832 | bytes 37748736 | tf_op jit(solution)/shard_map/pallas_call | solution.py:374
  554.3 5.9 place_columns.4
  560.3 179.9 %reduce_sum.21 = (f32[2,2,2,2,96,3072]{5,4,3,2,1,0:T(8,128)}, f32[8,1536]{1,0:T(8,128)}) custom-call(f32[2,2,2,2,96,3072]{5,4,3,2,1,0:T(8,128)} %bitcast.19, f32[8,1536]{1,0:T(8,128)} %maximum_maximum_fusion.e_ref), custom_call_target="tpu_custom_call" | custom-call | flops 1000000000 | bytes 37748736 | tf_op jit(solution)/shard_map/reduce_sum/pallas_call | solution.py:546
  740.2 1.6 slice_reduce_fusion
  743.1 16.8 %place_columns.7 = f32[1536,4608]{1,0:T(8,128)} custom-call(f32[1536,4608]{1,0:T(8,128)} %place_columns.6.refs_0_, f32[1536,3072]{1,0:T(8,128)} %bitcast.20), custom_call_target="tpu_custom_call", output_to_operand_aliasing={{}: (0, {})} | custom-call | flops 4718592 | bytes 37748736 | tf_op jit(solution)/shard_map/place_columns/pallas_call | solution.py:568
  759.9 5.9 copy.20
  (23 shorter events, 2.7 us)
Async XLA Ops:
  91.0 84.5 %all-to-all-start = ((bf16[8,256,1536]{2,1,0:T(8,128)(2,1)}), bf16[8,256,1536]{2,1,0:T(8,128)(2,1)}, u32[]{:S(2)}, u32[]{:S(2)}) async-start(bf16[8,256,1536]{2,1,0:T(8,128)(2,1)} %param.14), calls=%async_computation | async-start | bytes 12582912 | tf_op jit(solution)/shard_map/all_to_all | solution.py:591
  159.3 31.8 %slice-start = ((s8[4718592]{0:T(1024)(128)(4,1)}), s8[524288]{0:T(1024)(128)(4,1)S(1)}, s32[]{:S(2)}) async-start(s8[4718592]{0:T(1024)(128)(4,1)} %bitcast.26), calls=%async_computation.3 | async-start | bytes 1048576
  175.5 15.6 %slice-start.1 = ((s8[4718592]{0:T(1024)(128)(4,1)}), s8[4194304]{0:T(1024)(128)(4,1)S(1)}, s32[]{:S(2)}) async-start(s8[4718592]{0:T(1024)(128)(4,1)} %bitcast.26), calls=%async_computation.4 | async-start | bytes 8388608
  205.1 299.8 %all-to-all-start.1 = ((bf16[8,256,1536]{2,1,0:T(8,128)(2,1)}), bf16[8,256,1536]{2,1,0:T(8,128)(2,1)}, u32[]{:S(2)}, u32[]{:S(2)}) async-start(bf16[8,256,1536]{2,1,0:T(8,128)(2,1)} %bitcast.24), calls=%async_computation.1 | async-start | bytes 12582912 | tf_op jit(solution)/shard_map/all_to_all | solution.py:591
  504.9 4.0 copy-start.1
  504.9 4.3 copy-start
  504.9 255.0 %all-to-all-start.2 = ((bf16[8,256,1536]{2,1,0:T(8,128)(2,1)}), bf16[8,256,1536]{2,1,0:T(8,128)(2,1)}, u32[]{:S(2)}, u32[]{:S(2)}) async-start(bf16[8,256,1536]{2,1,0:T(8,128)(2,1)} %bitcast.23), calls=%async_computation.2 | async-start | bytes 12582912 | tf_op jit(solution)/shard_map/all_to_all | solution.py:591
  518.1 8.7 %copy-start.2 = (f32[1,1536]{1,0:T(1,128)S(1)}, f32[1,1536]{1,0:T(1,128)}, u32[]{:S(2)}) copy-start(f32[1,1536]{1,0:T(1,128)} %get-tuple-element.72) | copy-start | bytes 18436
